TPU v7x, 32 devices: a whole 2x2x4 slice. The times are simulated.
32 devices in a mesh: gx: 16 (over z, y, x), gy: 2 (over core).
Axes of the slice: x: 2, y: 2, z: 4, core: 2. Of those that a mesh axis runs over, the one named last changes fastest.
Arguments:
- sources: bfloat16 [2048, 8, 128], P(('gx', 'gy')), may hold values from -6 to 6
- owners: int32 [2048, 1], P(('gx', 'gy')), may hold values from 0 to 15; in each aligned block of 64 rows (0 to 63, 64 to 127, ...) at most 8 rows name the same one
- strip_rows: int32 [2048], P(('gx', 'gy')), may hold values from 0 to 255
- panel_counts: int32 [2048], P(('gx', 'gy')), may hold values from 1 to 128
- arrival_bins: int32 [4096, 4, 128], P('gx'), may hold values from 0 to 254
- arrival_fracs: float32 [4096, 4, 128], P('gx'), may hold values from 0 to 1
- gain_table: bfloat16 [4096, 8, 4, 1024], P('gx'), may hold values from -0.125 to 0.125
Outputs:
- signals: float32 [1024, 4, 256], P(('gx', 'gy'))
Inputs may be any that keep to these rules, and one draw needn't show every extreme that they name: `owners`: among the rows of one device, at most 8 strips name one patch, a bound that some block reaches.
All inputs are finite; a program needn't handle non-finite values.
Results may differ from a plain program's by a relative error of at most 0.0044.
Values may be sent and summed in bfloat16 or wider, within the bound.
A program may use at most 768 MiB of HBM per device.

v0:
```python
import jax
import jax.numpy as jnp
from jax import lax
from jax.sharding import PartitionSpec as P

NBIN = 256


def interp_weights(bin_ids, fractions):
    positions = jnp.arange(NBIN, dtype=jnp.int32)
    lower = jnp.where(
        positions[None, None, :] == bin_ids[:, :, None], 1.0 - fractions[:, :, None], 0.0
    )
    upper = jnp.where(
        positions[None, None, :] == bin_ids[:, :, None] + 1, fractions[:, :, None], 0.0
    )
    return (lower + upper).astype(jnp.bfloat16)


def bin_rows(row_rounded, bin_ids, fractions):
    blocks = bin_ids.shape[1]
    binned = []
    for block_index in range(blocks):
        weights = interp_weights(bin_ids[:, block_index, :], fractions[:, block_index, :])
        binned.append(
            jnp.einsum("rkp,rpb->rkb", row_rounded, weights, preferred_element_type=jnp.float32)
        )
    row_count, terms = (row_rounded.shape[0], row_rounded.shape[1])
    return jnp.stack(binned, axis=2).reshape(row_count * terms, blocks, NBIN).astype(jnp.bfloat16)


def on_device(sources, owners, strip_rows, panel_counts, arrival_bins, arrival_fracs, gain_table):
    strip_count, terms, panels = sources.shape
    shards = lax.axis_size("gx")
    columns = lax.axis_size("gy")
    capacity = 2 * strip_count // shards
    live_mask = (jnp.arange(panels, dtype=jnp.int32)[None, :] < panel_counts[:, None]).astype(
        jnp.bfloat16
    )
    masked = (sources * live_mask[:, None, :]).reshape(strip_count, terms * panels)
    targets = owners[:, 0]
    target_hot = (targets[:, None] == jnp.arange(shards, dtype=jnp.int32)[None, :]).astype(
        jnp.int32
    )
    order_in = jnp.sum((jnp.cumsum(target_hot, axis=0) - 1) * target_hot, axis=1)
    slot_of = targets * capacity + order_in
    placing = jnp.arange(shards * capacity, dtype=jnp.int32)[:, None] == slot_of[None, :]
    send_sources = jnp.dot(
        placing.astype(jnp.bfloat16), masked, preferred_element_type=jnp.float32
    ).astype(jnp.bfloat16)
    send_rows = jnp.sum(placing.astype(jnp.int32) * (strip_rows + 1)[None, :], axis=1) - 1
    got_sources, got_rows = (
        lax.all_to_all(send_sources, "gx", split_axis=0, concat_axis=0, tiled=True),
        lax.all_to_all(send_rows, "gx", split_axis=0, concat_axis=0, tiled=True),
    )
    rows_here = arrival_bins.shape[0]
    row_hot = (jnp.arange(rows_here, dtype=jnp.int32)[:, None] == got_rows[None, :]).astype(
        jnp.bfloat16
    )
    row_sources = jnp.dot(row_hot, got_sources, preferred_element_type=jnp.float32)
    blocks = arrival_bins.shape[1]
    observers = gain_table.shape[3]
    share = lax.psum_scatter(row_sources, "gy", scatter_dimension=0, tiled=True)
    share_rows = rows_here // columns
    first = lax.axis_index("gy") * share_rows
    row_rounded = share.astype(jnp.bfloat16).reshape(share_rows, terms, panels)
    own_bins = lax.dynamic_slice_in_dim(arrival_bins, first, share_rows, 0)
    own_fracs = lax.dynamic_slice_in_dim(arrival_fracs, first, share_rows, 0)
    arrived = bin_rows(row_rounded, own_bins, own_fracs)
    own_gains = lax.dynamic_slice_in_dim(gain_table, first, share_rows, 0).reshape(
        share_rows * terms, blocks, observers
    )
    return lax.psum_scatter(
        jnp.einsum("cot,cob->tob", own_gains, arrived, preferred_element_type=jnp.float32),
        ("gx", "gy"),
        scatter_dimension=0,
        tiled=True,
    )


def solution(mesh):
    placed = (
        P(("gx", "gy"), None, None),
        P(("gx", "gy"), None),
        P(("gx", "gy")),
        P(("gx", "gy")),
        P("gx", None, None),
        P("gx", None, None),
        P("gx", None, None, None),
    )
    return jax.shard_map(
        on_device,
        mesh=mesh,
        in_specs=placed,
        out_specs=P(("gx", "gy"), None, None),
        check_vma=False,
    )
```

profile of v0, /device:TPU:0, one launch (start us, length us, event | category | flops | bytes accessed | tf_op | source)
XLA Modules:
  0.0 274.6 jit_solution(13777596855906094471)
XLA Ops:
  6.5 0.7 fusion.31
  7.3 0.1 reduce_window_sum.11
  7.4 0.8 select_reduce_fusion.1
  8.2 0.7 multiply_add_fusion
  8.9 0.1 select_reduce_fusion
  9.0 0.7 sub.44
  9.7 8.3 %all-to-all-start = ((s32[16,8,1]{1,2,0:T(1,128)}), s32[16,8,1]{1,2,0:T(1,128)S(1)}, u32[]{:S(2)}, u32[]{:S(2)}) async-start(s32[16,8,1]{1,2,0:T(1,128)} %bitcast.1), calls=%async_computation | async-start | bytes 16384 | tf_op jit(solution)/shard_map/all_to_all | solution.py:54
  18.0 0.7 fusion.32
  18.8 0.9 broadcast_multiply_fusion
  19.7 1.0 fusion.25
  20.7 4.5 %all-to-all-done = s32[16,8,1]{1,2,0:T(1,128)S(1)} async-done(((s32[16,8,1]{1,2,0:T(1,128)}), s32[16,8,1]{1,2,0:T(1,128)S(1)}, u32[]{:S(2)}, u32[]{:S(2)}) %all-to-all-start) | async-done | bytes 544 | tf_op jit(solution)/shard_map/all_to_all | solution.py:54
  25.3 3.5 %all-to-all-start.1 = ((bf16[16,8,1024]{2,1,0:T(8,128)(2,1)}), bf16[16,8,1024]{2,1,0:T(8,128)(2,1)S(1)}, u32[]{:S(2)}, u32[]{:S(2)}) async-start(bf16[16,8,1024]{2,1,0:T(8,128)(2,1)} %fusion.25), calls=%async_computation.1 | async-start | bytes 524288 | tf_op jit(solution)/shard_map/all_to_all | solution.py:53
  28.8 0.0 reduce-scatter.2.cloned.1.call-start
  28.9 1.5 constant_dynamic-slice_fusion.4
  30.4 1.7 constant_dynamic-slice_fusion.3
  32.1 0.5 broadcast.102
  32.6 0.7 reduce.3
  33.3 0.1 eq.160
  33.4 3.9 %all-to-all-done.1 = bf16[16,8,1024]{2,1,0:T(8,128)(2,1)S(1)} async-done(((bf16[16,8,1024]{2,1,0:T(8,128)(2,1)}), bf16[16,8,1024]{2,1,0:T(8,128)(2,1)S(1)}, u32[]{:S(2)}, u32[]{:S(2)}) %all-to-all-start.1) | async-done | bytes 262176 | tf_op jit(solution)/shard_map/all_to_all | solution.py:53
  37.3 1.4 fusion.26
  38.6 0.0 reduce-scatter.2.cloned.1.call-update
  38.6 0.0 all-reduce.3.cloned.1.call-start
  38.8 8.4 %constant_dynamic-slice_fusion.5 = bf16[128,8,4,1024]{3,2,1,0:T(4,128)(2,1)} fusion(bf16[256,8,4,1024]{3,2,1,0:T(4,128)(2,1)} %param.13, s32[]{:T(128)S(6)} %select_n.30), kind=kLoop, calls=%fused_computation.66 | loop fusion | bytes 16777220 | tf_op jit(solution)/shard_map/dynamic_slice | solution.py:70
  47.2 0.0 reduce-scatter.2.cloned.1.call-done
  47.2 1.1 convert_bitcast_fusion
  48.3 14.7 %fusion.21 = bf16[1024,1,256]{2,0,1:T(8,128)(2,1)S(1)} fusion(bf16[128,8,128]{2,1,0:T(8,128)(2,1)S(1)} %bitcast.58, f32[128,128]{1,0:T(8,128)S(1)} %bitcast.77, s32[128,128]{1,0:T(8,128)S(1)} %broadcast_add_fusion.3, f32[128,128]{1,0:T(8,128)S(1)} %broadcast_subtract_fusion.3, s32[128,128]{1,0:T(8,128)S(1)} %bitcast.75), kind=kOutput, calls=%fused_computation.31 | convolution fusion | flops 92536832 | bytes 1048576 | tf_op jit(solution)/shard_map/rkp,rpb->rkb/dot_general | solution.py:26
  63.0 0.2 copy.52
  63.2 14.7 %fusion.22 = bf16[1024,1,256]{2,0,1:T(8,128)(2,1)S(1)} fusion(bf16[128,8,128]{2,1,0:T(8,128)(2,1)S(1)} %bitcast.59, f32[128,128]{1,0:T(8,128)S(1)} %bitcast.73, s32[128,128]{1,0:T(8,128)S(1)} %broadcast_add_fusion.2, f32[128,128]{1,0:T(8,128)S(1)} %broadcast_subtract_fusion.2, s32[128,128]{1,0:T(8,128)S(1)} %bitcast.71), kind=kOutput, calls=%fused_computation.32 | convolution fusion | flops 92536832 | bytes 1048576 | tf_op jit(solution)/shard_map/rkp,rpb->rkb/dot_general | solution.py:26
  78.0 0.2 copy.53
  78.2 14.7 %fusion.23 = bf16[1024,1,256]{2,0,1:T(8,128)(2,1)S(1)} fusion(bf16[128,8,128]{2,1,0:T(8,128)(2,1)S(1)} %bitcast.60, f32[128,128]{1,0:T(8,128)S(1)} %bitcast.69, s32[128,128]{1,0:T(8,128)S(1)} %broadcast_add_fusion.1, f32[128,128]{1,0:T(8,128)S(1)} %broadcast_subtract_fusion.1, s32[128,128]{1,0:T(8,128)S(1)} %bitcast.67), kind=kOutput, calls=%fused_computation.33 | convolution fusion | flops 92536832 | bytes 1048576 | tf_op jit(solution)/shard_map/rkp,rpb->rkb/dot_general | solution.py:26
  92.9 0.2 copy.54
  93.1 14.7 %fusion.24 = bf16[1024,1,256]{2,0,1:T(8,128)(2,1)S(1)} fusion(bf16[128,8,128]{2,1,0:T(8,128)(2,1)S(1)} %bitcast.61, f32[128,128]{1,0:T(8,128)S(1)} %bitcast.65, s32[128,128]{1,0:T(8,128)S(1)} %broadcast_add_fusion, f32[128,128]{1,0:T(8,128)S(1)} %broadcast_subtract_fusion, s32[128,128]{1,0:T(8,128)S(1)} %bitcast.63), kind=kOutput, calls=%fused_computation.34 | convolution fusion | flops 92536832 | bytes 1048576 | tf_op jit(solution)/shard_map/rkp,rpb->rkb/dot_general | solution.py:26
  107.8 0.2 copy.55
  108.0 10.9 %fusion.7 = f32[1024,4,256]{0,2,1:T(8,128)} fusion(bf16[128,8,4,1024]{3,2,1,0:T(4,128)(2,1)} %constant_dynamic-slice_fusion.5, bf16[1024,1,256]{0,2,1:T(8,128)(2,1)S(1)} %copy.55, bf16[1024,1,256]{0,2,1:T(8,128)(2,1)S(1)} %copy.54, bf16[1024,1,256]{0,2,1:T(8,128)(2,1)S(1)} %copy.53, bf16[1024,1,256]{0,2,1:T(8,128)(2,1)S(1)} %copy.52), kind=kOutput, calls=%fused_computation.19 | convolution fusion | flops 2150629376 | bytes 14680064 | tf_op jit(solution)/shard_map/cot,cob->tob/dot_general | solution.py:74
  118.9 5.2 %copy.57 = f32[1024,4,256]{2,1,0:T(4,128)} copy(f32[1024,4,256]{0,2,1:T(8,128)} %fusion.7) | data formatting | bytes 8388608 | tf_op jit(solution)/shard_map/cot,cob->tob/transpose | solution.py:74
  124.2 0.0 all-reduce.3.cloned.1.call-update
  124.2 142.0 %all-reduce.3.cloned.1.call-done = f32[1024,4,256]{2,1,0:T(4,128)} async-done(((f32[1024,4,256]{2,1,0:T(4,128)}), f32[1024,4,256]{2,1,0:T(4,128)}) %all-reduce.3.cloned.1.call-update) | async-done | bytes 4194320
  266.2 1.6 constant_dynamic-slice_fusion.9
  (10 shorter events, 0.1 us)
Async XLA Ops:
  9.7 15.6 %all-to-all-start = ((s32[16,8,1]{1,2,0:T(1,128)}), s32[16,8,1]{1,2,0:T(1,128)S(1)}, u32[]{:S(2)}, u32[]{:S(2)}) async-start(s32[16,8,1]{1,2,0:T(1,128)} %bitcast.1), calls=%async_computation | async-start | bytes 16384 | tf_op jit(solution)/shard_map/all_to_all | solution.py:54
  25.3 12.0 %all-to-all-start.1 = ((bf16[16,8,1024]{2,1,0:T(8,128)(2,1)}), bf16[16,8,1024]{2,1,0:T(8,128)(2,1)S(1)}, u32[]{:S(2)}, u32[]{:S(2)}) async-start(bf16[16,8,1024]{2,1,0:T(8,128)(2,1)} %fusion.25), calls=%async_computation.1 | async-start | bytes 524288 | tf_op jit(solution)/shard_map/all_to_all | solution.py:53
  28.8 18.4 %reduce-scatter.2.cloned.1.call-start = ((), (), s32[]{:S(2)}) async-start(), calls=%async_computation.3 | async-start | bytes 1572864 | tf_op jit(solution)/shard_map/reduce_scatter | solution.py:63
  38.6 227.5 %all-reduce.3.cloned.1.call-start = ((), (), s32[]{:S(2)}) async-start(), calls=%async_computation.4 | async-start | bytes 8388608
Sparse Core Ops, SparseCore 0:
  38.8 6.4 reduce-scatter.1
  124.3 141.8 all-reduce.2
where the time goes:
time: 275 us
  waiting for transfers between devices  150 us (55%)
  matrix products  72.1 us (26%)
  local copies, waits for them, and re-layouts  20.6 us (7%)
  between operations  13.6 us (5%)
  starting transfers between devices  12 us (4%)
  other arithmetic  5.91 us (2%)
    unnamed x3, waiting for transfers between devices  142 us
    dot_general x4, matrix products, bin_rows(): jnp.einsum('rkp,rpb->rkb', row_rounded, weights, preferred_element_type=j...  58.9 us
    dot_general x1, matrix products, on_device(): jnp.einsum('cot,cob->tob', own_gains, arrived, preferred_element_type=jnp...  10.9 us
    dynamic_slice x1, local copies, waits for them, and re-layouts, on_device(): lax.dynamic_slice_in_dim(gain_table, first, share_rows, 0)  8.35 us
    all_to_all x1, starting transfers between devices, on_device(): lax.all_to_all(send_rows, 'gx', split_axis=0, concat_axis=0, tiled=True)  8.34 us
  transfers between devices with their start and end apart: 4, of which 3 were waited for; matrix products, arithmetic and copies ran while one was open for 6% of the time, Pallas kernels for 0%

commit v1 on v0

v1 whole, which is shorter than its diff:
```python
import functools

import jax
import jax.numpy as jnp
from jax import lax
from jax.experimental import pallas as pl
from jax.experimental.pallas import tpu as pltpu
from jax.sharding import PartitionSpec as P

NBIN = 256


def bin_kernel(block_ref, src_ref, bins_ref, fracs_ref, out_ref):
    block = block_ref[0]
    pairs = src_ref.shape[0] // 16
    panels = src_ref.shape[1]
    low = lax.broadcasted_iota(jnp.int32, (16, panels), 0) < 8
    spots = lax.broadcasted_iota(jnp.int32, (NBIN, panels), 0).astype(jnp.float32).astype(jnp.bfloat16)

    def weights_of(row):
        bins = bins_ref[row, pl.ds(block, 1), :].astype(jnp.float32)
        fracs = fracs_ref[row, pl.ds(block, 1), :]

        def spread(v):
            return jnp.broadcast_to(v, (NBIN, panels)).astype(jnp.bfloat16)

        first, second = spread(bins), spread(bins + 1.0)
        return jnp.where(
            spots == first,
            spread(1.0 - fracs),
            jnp.where(spots == second, spread(fracs), jnp.zeros((), jnp.bfloat16)),
        )

    def step(i, carry):
        both = src_ref[pl.ds(pl.multiple_of(i * 16, 16), 16), :].astype(jnp.float32)
        top = jnp.where(low, both, 0.0).astype(jnp.bfloat16)
        bottom = jnp.where(low, 0.0, both).astype(jnp.bfloat16)
        lhs = jnp.concatenate([top, bottom], axis=1)
        weights = jnp.concatenate([weights_of(2 * i), weights_of(2 * i + 1)], axis=1)
        got = lax.dot_general(
            lhs, weights, (((1,), (1,)), ((), ())), preferred_element_type=jnp.float32
        )
        out_ref[pl.ds(pl.multiple_of(i * 16, 16), 16), :] = got.astype(jnp.bfloat16)
        return carry

    lax.fori_loop(0, pairs, step, 0, unroll=4)


def bin_rows(block, src, bins, fracs):
    rows = src.shape[0]
    return pl.pallas_call(
        bin_kernel,
        out_shape=jax.ShapeDtypeStruct((rows, NBIN), jnp.bfloat16),
        in_specs=[
            pl.BlockSpec(memory_space=pltpu.SMEM),
            pl.BlockSpec(memory_space=pltpu.VMEM),
            pl.BlockSpec(memory_space=pltpu.VMEM),
            pl.BlockSpec(memory_space=pltpu.VMEM),
        ],
        out_specs=pl.BlockSpec(memory_space=pltpu.VMEM),
        name="bin_rows",
        cost_estimate=pl.CostEstimate(flops=rows * 2 * 256 * 256, bytes_accessed=rows * 1000, transcendentals=0),
    )(block, src, bins, fracs)


def on_device(sources, owners, strip_rows, panel_counts, arrival_bins, arrival_fracs, gain_table):
    strip_count, terms, panels = sources.shape
    shards = lax.axis_size("gx")
    columns = lax.axis_size("gy")
    capacity = 2 * strip_count // shards
    blocks = arrival_bins.shape[1]
    observers = gain_table.shape[3]
    rows_here = arrival_bins.shape[0]
    live_mask = (jnp.arange(panels, dtype=jnp.int32)[None, :] < panel_counts[:, None]).astype(
        jnp.bfloat16
    )
    masked = (sources * live_mask[:, None, :]).reshape(strip_count, terms * panels)
    lane = jnp.arange(128, dtype=jnp.int32)[None, :]
    coded = jnp.where(
        lane == 0,
        (strip_rows // 128)[:, None],
        jnp.where(lane == 1, (strip_rows % 128)[:, None], jnp.where(lane == 2, 1, 0)),
    ).astype(jnp.bfloat16)
    payload = jnp.concatenate([masked, coded], axis=1)
    targets = owners[:, 0]
    earlier = (
        jnp.arange(strip_count, dtype=jnp.int32)[None, :]
        < jnp.arange(strip_count, dtype=jnp.int32)[:, None]
    )
    order_in = jnp.sum(
        jnp.where(earlier & (targets[None, :] == targets[:, None]), 1, 0).astype(jnp.int32), axis=1
    )
    slot_of = targets * capacity + order_in
    placing = jnp.arange(shards * capacity, dtype=jnp.int32)[:, None] == slot_of[None, :]
    send = jnp.dot(
        placing.astype(jnp.bfloat16), payload, preferred_element_type=jnp.float32
    ).astype(jnp.bfloat16)
    got = lax.all_to_all(send, "gx", split_axis=0, concat_axis=0, tiled=True)
    got = lax.all_gather(got, "gy", axis=0, tiled=True)
    codes = got[:, terms * panels :].astype(jnp.int32)
    got_rows = jnp.where(codes[:, 2] > 0, codes[:, 0] * 128 + codes[:, 1], -1)
    row_hot = (jnp.arange(rows_here, dtype=jnp.int32)[:, None] == got_rows[None, :]).astype(
        jnp.bfloat16
    )
    row_sources = jnp.dot(
        row_hot, got[:, : terms * panels], preferred_element_type=jnp.float32
    ).astype(jnp.bfloat16)
    src = row_sources.reshape(rows_here * terms, panels)
    per = blocks // columns
    first = lax.axis_index("gy") * per
    gains = lax.dynamic_slice_in_dim(gain_table, first, per, 2)
    sums = []
    share = observers // (shards * columns)
    for o in range(per):
        block = (first + o).astype(jnp.int32).reshape(1)
        arrived = bin_rows(block, src, arrival_bins, arrival_fracs)
        partial = jnp.einsum(
            "ct,cb->tb",
            gains[:, :, o, :].reshape(rows_here * terms, observers),
            arrived,
            preferred_element_type=jnp.float32,
        ).astype(jnp.bfloat16)
        parts = lax.all_to_all(partial, ("gx", "gy"), split_axis=0, concat_axis=0, tiled=True)
        sums.append(
            jnp.sum(parts.reshape(shards, columns, share, NBIN).astype(jnp.float32), axis=0)
        )
    return jnp.stack(sums, axis=1).transpose(2, 0, 1, 3).reshape(share, blocks, NBIN)


def solution(mesh):
    placed = (
        P(("gx", "gy"), None, None),
        P(("gx", "gy"), None),
        P(("gx", "gy")),
        P(("gx", "gy")),
        P("gx", None, None),
        P("gx", None, None),
        P("gx", None, None, None),
    )
    return jax.shard_map(
        on_device,
        mesh=mesh,
        in_specs=placed,
        out_specs=P(("gx", "gy"), None, None),
        check_vma=False,
    )
```

time: 275 us -> 105 us (0.38)
  waiting for transfers between devices: 150 us -> 15.5 us
  matrix products: 72.1 us -> 15.4 us
  Pallas kernels: 0 us -> 21.8 us
  between operations: 13.6 us -> 0.11 us
  starting transfers between devices: 12 us -> 20.1 us
  local copies, waits for them, and re-layouts: 20.6 us -> 25.5 us
    unnamed x3 -> x0, waiting for transfers between devices: 142 us -> none
    dot_general x7 -> x4, matrix products: 72.1 us -> 15.4 us  [the longest x2 14.2 us: on_device(): jnp.einsum('ct,cb->tb', gains[:, :, o, :].reshape(rows_here * terms, obse...]
    pallas_call x0 -> x2, Pallas kernels: none -> 21.8 us  [bin_rows(): pl.pallas_call(bin_kernel, out_shape=jax.ShapeDtypeStruct((rows, NBIN), j...]
    slice x2 -> x1, local copies, waits for them, and re-layouts: 3.24 us -> 23.7 us  [on_device(): gains[:, :, o, :].reshape(rows_here * terms, observers)]
    dynamic_slice x1 -> x0, local copies, waits for them, and re-layouts: 8.35 us -> none  [on_device(): lax.dynamic_slice_in_dim(gain_table, first, share_rows, 0)]
    all_to_all x2 -> x3, starting transfers between devices: 11.9 us -> 20.1 us  [the longest x2 11.7 us: on_device(): lax.all_to_all(partial, ('gx', 'gy'), split_axis=0, concat_axis=0, tiled=...]
    all_to_all x2 -> x3, waiting for transfers between devices: 8.41 us -> 15.5 us  [the longest x2 15.5 us: on_device(): lax.all_to_all(partial, ('gx', 'gy'), split_axis=0, concat_axis=0, tiled=...]
    transpose x1, local copies, waits for them, and re-layouts: 5.24 us -> 0.01 us  [on_device(): jnp.stack(sums, axis=1).transpose(2, 0, 1, 3).reshape(share, blocks, NBIN)]
  transfers between devices with their start and end apart: 4 -> 3, of which waited for: 3 -> 1; matrix products, arithmetic and copies ran while one was open for 6% -> 29% of each run, Pallas kernels for 0% -> 10%
where the time goes in v1:
time: 105 us
  local copies, waits for them, and re-layouts  25.5 us (24%)
  Pallas kernels  21.8 us (21%)
  starting transfers between devices  20.1 us (19%)
  waiting for transfers between devices  15.5 us (15%)
  matrix products  15.4 us (15%)
  other arithmetic  4.38 us (4%)
  blocking collectives  2.23 us (2%)
    slice x1, local copies, waits for them, and re-layouts, on_device(): gains[:, :, o, :].reshape(rows_here * terms, observers)  23.7 us
    pallas_call x2, Pallas kernels, bin_rows(): pl.pallas_call(bin_kernel, out_shape=jax.ShapeDtypeStruct((rows, NBIN), j...  21.8 us
    all_to_all x2, waiting for transfers between devices, on_device(): lax.all_to_all(partial, ('gx', 'gy'), split_axis=0, concat_axis=0, tiled=...  15.5 us
    dot_general x2, matrix products, on_device(): jnp.einsum('ct,cb->tb', gains[:, :, o, :].reshape(rows_here * terms, obse...  14.2 us
    all_to_all x2, starting transfers between devices, on_device(): lax.all_to_all(partial, ('gx', 'gy'), split_axis=0, concat_axis=0, tiled=...  11.7 us
    all_to_all x1, starting transfers between devices, on_device(): got = lax.all_to_all(send, 'gx', split_axis=0, concat_axis=0, tiled=True)  8.35 us
    all_gather x1, blocking collectives, on_device(): got = lax.all_gather(got, 'gy', axis=0, tiled=True)  2.23 us
  transfers between devices with their start and end apart: 3, of which 1 were waited for; matrix products, arithmetic and copies ran while one was open for 29% of the time, Pallas kernels for 10%

profile of v1, /device:TPU:0, one launch (start us, length us, event | category | flops | bytes accessed | tf_op | source)
XLA Modules:
  0.0 105.0 jit_solution(13986246355079080229)
XLA Ops:
  0.0 0.7 and_select_fusion.1
  0.7 0.7 fusion.14
  1.4 0.9 broadcast_multiply_fusion
  2.4 0.9 select_reduce_fusion
  3.3 0.7 multiply_add_fusion
  3.9 0.1 select_convert_fusion
  4.0 0.9 fusion.2
  5.0 8.3 %all-to-all-start = ((bf16[16,8,1152]{2,1,0:T(8,128)(2,1)}), bf16[16,8,1152]{2,1,0:T(8,128)(2,1)S(1)}, u32[]{:S(2)}, u32[]{:S(2)}) async-start(bf16[16,8,1152]{2,1,0:T(8,128)(2,1)} %fusion.2), calls=%async_computation | async-start | bytes 589824 | tf_op jit(solution)/shard_map/all_to_all | solution.py:98
  13.3 23.7 %constant_dynamic-slice_fusion = (bf16[256,8,1,1024]{3,2,1,0:T(2,128)(2,1)}, bf16[256,8,1,1024]{3,2,1,0:T(2,128)(2,1)}) fusion(bf16[256,8,4,1024]{3,2,1,0:T(4,128)(2,1)} %param.13, s32[]{:T(128)S(6)} %select_n.47, s32[]{:T(128)S(6)} %add.34), kind=kLoop, calls=%fused_computation.43 | loop fusion | bytes 16777224 | tf_op jit(solution)/shard_map/slice | solution.py:119
  37.0 0.0 all-to-all-done
  37.0 2.2 %all_gather.3 = bf16[256,1152]{1,0:T(8,128)(2,1)S(1)} all-gather(bf16[128,1152]{1,0:T(8,128)(2,1)S(1)} %bitcast.36), channel_id=1, replica_groups=mesh['gx'=16,'gy'=2] {'gy'}, dimensions={0}, use_global_device_ids=true | all-gather | bytes 884736 | tf_op jit(solution)/shard_map/all_gather | solution.py:99
  39.2 0.2 fusion.10
  39.4 0.3 convolution_convert_fusion.1
  39.8 1.0 reshape.100.src_ref
  40.8 10.9 %bin_rows.2 = bf16[2048,256]{1,0:T(8,128)(2,1)} custom-call(s32[1]{0:T(128)} %bitcast.1.block_ref, bf16[2048,128]{1,0:T(8,128)(2,1)} %reshape.100.src_ref, s32[256,4,128]{2,1,0:T(4,128)} %bins_ref.3, f32[256,4,128]{2,1,0:T(4,128)} %fracs_ref.3), custom_call_target="tpu_custom_call" | custom-call | flops 268435456 | bytes 2048000 | tf_op jit(solution)/shard_map/bin_rows/pallas_call | solution.py:51
  51.7 7.1 %fusion.3 = bf16[1024,256]{1,0:T(8,128)(2,1)} fusion(bf16[2048,256]{1,0:T(8,128)(2,1)} %bin_rows.2, bf16[256,8,1,1024]{3,2,1,0:T(2,128)(2,1)} %get-tuple-element.5), kind=kOutput, calls=%fused_computation.7 | convolution fusion | flops 1074003968 | bytes 5767168 | tf_op jit(solution)/shard_map/ct,cb->tb/dot_general | solution.py:117
  58.8 5.9 %all-to-all-start.1 = ((bf16[32,32,256]{2,1,0:T(8,128)(2,1)}), bf16[32,32,256]{2,1,0:T(8,128)(2,1)S(1)}, u32[]{:S(2)}, u32[]{:S(2)}) async-start(bf16[32,32,256]{2,1,0:T(8,128)(2,1)} %bitcast.5), calls=%async_computation.1 | async-start | bytes 1048576 | tf_op jit(solution)/shard_map/all_to_all | solution.py:123
  64.7 11.0 %bin_rows.3 = bf16[2048,256]{1,0:T(8,128)(2,1)} custom-call(s32[1]{0:T(128)} %bitcast.9.block_ref, bf16[2048,128]{1,0:T(8,128)(2,1)} %reshape.100.src_ref, s32[256,4,128]{2,1,0:T(4,128)} %bins_ref.3, f32[256,4,128]{2,1,0:T(4,128)} %fracs_ref.3), custom_call_target="tpu_custom_call" | custom-call | flops 268435456 | bytes 2048000 | tf_op jit(solution)/shard_map/bin_rows/pallas_call | solution.py:51
  75.6 7.1 %fusion.4 = bf16[1024,256]{1,0:T(8,128)(2,1)} fusion(bf16[2048,256]{1,0:T(8,128)(2,1)} %bin_rows.3, bf16[256,8,1,1024]{3,2,1,0:T(2,128)(2,1)} %get-tuple-element.6), kind=kOutput, calls=%fused_computation.8 | convolution fusion | flops 1074003968 | bytes 5767168 | tf_op jit(solution)/shard_map/ct,cb->tb/dot_general | solution.py:117
  82.7 0.0 all-to-all-done.1
  82.7 5.8 %all-to-all-start.2 = ((bf16[32,32,256]{2,1,0:T(8,128)(2,1)}), bf16[32,32,256]{2,1,0:T(8,128)(2,1)S(1)}, u32[]{:S(2)}, u32[]{:S(2)}) async-start(bf16[32,32,256]{2,1,0:T(8,128)(2,1)} %bitcast.10), calls=%async_computation.2 | async-start | bytes 1048576 | tf_op jit(solution)/shard_map/all_to_all | solution.py:123
  88.5 0.1 convert_reduce_fusion.1
  88.6 15.5 %all-to-all-done.2 = bf16[32,32,256]{2,1,0:T(8,128)(2,1)S(1)} async-done(((bf16[32,32,256]{2,1,0:T(8,128)(2,1)}), bf16[32,32,256]{2,1,0:T(8,128)(2,1)S(1)}, u32[]{:S(2)}, u32[]{:S(2)}) %all-to-all-start.2) | async-done | bytes 524320 | tf_op jit(solution)/shard_map/all_to_all | solution.py:123
  104.2 0.1 convert_reduce_fusion
  104.3 0.7 copy.17
  (6 shorter events, 0.1 us)
Async XLA Ops:
  5.0 32.0 %all-to-all-start = ((bf16[16,8,1152]{2,1,0:T(8,128)(2,1)}), bf16[16,8,1152]{2,1,0:T(8,128)(2,1)S(1)}, u32[]{:S(2)}, u32[]{:S(2)}) async-start(bf16[16,8,1152]{2,1,0:T(8,128)(2,1)} %fusion.2), calls=%async_computation | async-start | bytes 589824 | tf_op jit(solution)/shard_map/all_to_all | solution.py:98
  58.8 23.9 %all-to-all-start.1 = ((bf16[32,32,256]{2,1,0:T(8,128)(2,1)}), bf16[32,32,256]{2,1,0:T(8,128)(2,1)S(1)}, u32[]{:S(2)}, u32[]{:S(2)}) async-start(bf16[32,32,256]{2,1,0:T(8,128)(2,1)} %bitcast.5), calls=%async_computation.1 | async-start | bytes 1048576 | tf_op jit(solution)/shard_map/all_to_all | solution.py:123
  82.7 21.5 %all-to-all-start.2 = ((bf16[32,32,256]{2,1,0:T(8,128)(2,1)}), bf16[32,32,256]{2,1,0:T(8,128)(2,1)S(1)}, u32[]{:S(2)}, u32[]{:S(2)}) async-start(bf16[32,32,256]{2,1,0:T(8,128)(2,1)} %bitcast.10), calls=%async_computation.2 | async-start | bytes 1048576 | tf_op jit(solution)/shard_map/all_to_all | solution.py:123

commit v2 on v1

--- a/solution.py
+++ b/solution.py
@@ -63,6 +63,13 @@
     )(block, src, bins, fracs)
 
 
+def gained(block, gain_table, arrived):
+    gains = gain_table[:, :, block, :].reshape(arrived.shape[0], gain_table.shape[3])
+    return jnp.einsum("ct,cb->tb", gains, arrived, preferred_element_type=jnp.float32).astype(
+        jnp.bfloat16
+    )
+
+
 def on_device(sources, owners, strip_rows, panel_counts, arrival_bins, arrival_fracs, gain_table):
     strip_count, terms, panels = sources.shape
     shards = lax.axis_size("gx")
@@ -108,18 +115,17 @@
     src = row_sources.reshape(rows_here * terms, panels)
     per = blocks // columns
     first = lax.axis_index("gy") * per
-    gains = lax.dynamic_slice_in_dim(gain_table, first, per, 2)
     sums = []
     share = observers // (shards * columns)
     for o in range(per):
         block = (first + o).astype(jnp.int32).reshape(1)
         arrived = bin_rows(block, src, arrival_bins, arrival_fracs)
-        partial = jnp.einsum(
-            "ct,cb->tb",
-            gains[:, :, o, :].reshape(rows_here * terms, observers),
+        partial = lax.switch(
+            lax.axis_index("gy"),
+            [functools.partial(gained, column * per + o) for column in range(columns)],
+            gain_table,
             arrived,
-            preferred_element_type=jnp.float32,
-        ).astype(jnp.bfloat16)
+        )
         parts = lax.all_to_all(partial, ("gx", "gy"), split_axis=0, concat_axis=0, tiled=True)
         sums.append(
             jnp.sum(parts.reshape(shards, columns, share, NBIN).astype(jnp.float32), axis=0)

time: 105 us -> 102 us (0.971)
  waiting for transfers between devices: 15.5 us -> 26.2 us
  matrix products: 15.4 us -> 5.52 us
  starting transfers between devices: 20.1 us -> 16.8 us
  Pallas kernels: 21.8 us -> 19.7 us
    another operation x0 -> x2, local copies, waits for them, and re-layouts: none -> 24.7 us
    slice x1 -> x0, local copies, waits for them, and re-layouts: 23.7 us -> none  [on_device(): gains[:, :, o, :].reshape(rows_here * terms, observers)]
    all_to_all x1, waiting for transfers between devices: 0.01 us -> 10.7 us  [on_device(): got = lax.all_to_all(send, 'gx', split_axis=0, concat_axis=0, tiled=True)]
    dot_general x2, matrix products: 14.2 us -> 4.28 us  [gained(): jnp.einsum('ct,cb->tb', gains, arrived, preferred_element_type=jnp.float32)]
    all_to_all x2, starting transfers between devices: 11.7 us -> 8.44 us  [on_device(): lax.all_to_all(partial, ('gx', 'gy'), split_axis=0, concat_axis=0, tiled=...]
    pallas_call x2, Pallas kernels: 21.8 us -> 19.7 us  [bin_rows(): pl.pallas_call(bin_kernel, out_shape=jax.ShapeDtypeStruct((rows, NBIN), j...]
  transfers between devices with their start and end apart: 3 -> 3, of which waited for: 1 -> 2; matrix products, arithmetic and copies ran while one was open for 29% -> 14% of each run, Pallas kernels for 10% -> 10%
where the time goes in v2:
time: 102 us; the launch traced here: 101 us
  local copies, waits for them, and re-layouts  26.5 us (26%)
  waiting for transfers between devices  26.2 us (26%)
  Pallas kernels  19.7 us (19%)
  starting transfers between devices  16.8 us (16%)
  matrix products  5.52 us (5%)
  other arithmetic  4.38 us (4%)
  blocking collectives  2.22 us (2%)
    another operation x2, local copies, waits for them, and re-layouts  24.7 us
    pallas_call x2, Pallas kernels, bin_rows(): pl.pallas_call(bin_kernel, out_shape=jax.ShapeDtypeStruct((rows, NBIN), j...  19.7 us
    all_to_all x2, waiting for transfers between devices, on_device(): lax.all_to_all(partial, ('gx', 'gy'), split_axis=0, concat_axis=0, tiled=...  15.5 us
    all_to_all x1, waiting for transfers between devices, on_device(): got = lax.all_to_all(send, 'gx', split_axis=0, concat_axis=0, tiled=True)  10.7 us
    all_to_all x2, starting transfers between devices, on_device(): lax.all_to_all(partial, ('gx', 'gy'), split_axis=0, concat_axis=0, tiled=...  8.44 us
    all_to_all x1, starting transfers between devices, on_device(): got = lax.all_to_all(send, 'gx', split_axis=0, concat_axis=0, tiled=True)  8.34 us
    dot_general x2, matrix products, gained(): jnp.einsum('ct,cb->tb', gains, arrived, preferred_element_type=jnp.float32)  4.28 us
    all_gather x1, blocking collectives, on_device(): got = lax.all_gather(got, 'gy', axis=0, tiled=True)  2.22 us
  transfers between devices with their start and end apart: 3, of which 2 were waited for; matrix products, arithmetic and copies ran while one was open for 14% of the time, Pallas kernels for 10%

profile of v2, /device:TPU:0, one launch (start us, length us, event | category | flops | bytes accessed | tf_op | source)
XLA Modules:
  0.0 101.4 jit_solution(9074223080902458986)
XLA Ops:
  0.0 0.9 select_reduce_fusion
  0.9 0.7 multiply_add_fusion
  1.6 0.7 and_select_fusion.1
  2.3 0.7 fusion.14
  3.0 0.9 broadcast_multiply_fusion
  3.9 0.1 select_convert_fusion
  4.0 0.9 fusion.4
  5.0 8.3 %all-to-all-start = ((bf16[16,8,1152]{2,1,0:T(8,128)(2,1)}), bf16[16,8,1152]{2,1,0:T(8,128)(2,1)S(1)}, u32[]{:S(2)}, u32[]{:S(2)}) async-start(bf16[16,8,1152]{2,1,0:T(8,128)(2,1)} %fusion.4), calls=%async_computation | async-start | bytes 589824 | tf_op jit(solution)/shard_map/all_to_all | solution.py:105
  13.3 10.7 %all-to-all-done = bf16[16,8,1152]{2,1,0:T(8,128)(2,1)S(1)} async-done(((bf16[16,8,1152]{2,1,0:T(8,128)(2,1)}), bf16[16,8,1152]{2,1,0:T(8,128)(2,1)S(1)}, u32[]{:S(2)}, u32[]{:S(2)}) %all-to-all-start) | async-done | bytes 294944 | tf_op jit(solution)/shard_map/all_to_all | solution.py:105
  24.0 2.2 %all_gather.3 = bf16[256,1152]{1,0:T(8,128)(2,1)S(1)} all-gather(bf16[128,1152]{1,0:T(8,128)(2,1)S(1)} %bitcast.40), channel_id=1, replica_groups=mesh['gx'=16,'gy'=2] {'gy'}, dimensions={0}, use_global_device_ids=true | all-gather | bytes 884736 | tf_op jit(solution)/shard_map/all_gather | solution.py:106
  26.2 0.2 fusion.10
  26.4 0.3 convolution_convert_fusion.1
  26.8 1.0 reshape.100.src_ref
  27.8 9.9 %bin_rows.3 = bf16[2048,256]{1,0:T(8,128)(2,1)S(1)} custom-call(s32[1]{0:T(128)} %bitcast.11.block_ref, bf16[2048,128]{1,0:T(8,128)(2,1)} %reshape.100.src_ref, s32[256,4,128]{2,1,0:T(4,128)} %bins_ref.3, f32[256,4,128]{2,1,0:T(4,128)} %fracs_ref.3), custom_call_target="tpu_custom_call" | custom-call | flops 268435456 | bytes 2048000 | tf_op jit(solution)/shard_map/bin_rows/pallas_call | solution.py:51
  37.6 14.5 %conditional.5 = (bf16[1024,256]{1,0:T(8,128)(2,1)}) conditional(s32[]{:T(128)} %clamp.4, (bf16[256,8,4,1024]{3,2,1,0:T(4,128)(2,1)}, bf16[2048,256]{1,0:T(8,128)(2,1)S(1)}) %tuple.24, (bf16[256,8,4,1024]{3,2,1,0:T(4,128)(2,1)}, bf16[2048,256]{1,0:T(8,128)(2,1)S(1)}) %tuple.24), branch_computations={%region_4.5_spmd, %region_5.6_spmd} | conditional | flops 1073741824 | bytes 39321608
  37.6 12.4 %copy.29 = bf16[256,8,4,1024]{3,1,0,2:T(8,128)(2,1)S(1)} copy(bf16[256,8,4,1024]{3,2,1,0:T(4,128)(2,1)} %get-tuple-element.75) | data formatting | bytes 33554432 | tf_op jit(solution)/shard_map
  50.0 2.2 %fusion.2 = bf16[1024,256]{1,0:T(8,128)(2,1)} fusion(bf16[2048,256]{1,0:T(8,128)(2,1)S(1)} %get-tuple-element.36, bf16[256,8,4,1024]{3,1,0,2:T(8,128)(2,1)S(1)} %copy.29), kind=kOutput, calls=%fused_computation.5 | convolution fusion | flops 1073741824 | bytes 5767168 | tf_op jit(solution)/shard_map/cond/branch_0_fun/ct,cb->tb/dot_general | solution.py:68
  52.1 2.6 %all-to-all-start.2 = ((bf16[32,32,256]{2,1,0:T(8,128)(2,1)}), bf16[32,32,256]{2,1,0:T(8,128)(2,1)S(1)}, u32[]{:S(2)}, u32[]{:S(2)}) async-start(bf16[32,32,256]{2,1,0:T(8,128)(2,1)} %bitcast.12), calls=%async_computation.2 | async-start | bytes 1048576 | tf_op jit(solution)/shard_map/all_to_all | solution.py:129
  54.7 9.9 %bin_rows.2 = bf16[2048,256]{1,0:T(8,128)(2,1)S(1)} custom-call(s32[1]{0:T(128)} %bitcast.4.block_ref, bf16[2048,128]{1,0:T(8,128)(2,1)} %reshape.100.src_ref, s32[256,4,128]{2,1,0:T(4,128)} %bins_ref.3, f32[256,4,128]{2,1,0:T(4,128)} %fracs_ref.3), custom_call_target="tpu_custom_call" | custom-call | flops 268435456 | bytes 2048000 | tf_op jit(solution)/shard_map/bin_rows/pallas_call | solution.py:51
  64.6 14.5 %conditional.4 = (bf16[1024,256]{1,0:T(8,128)(2,1)}) conditional(s32[]{:T(128)} %clamp.4, (bf16[256,8,4,1024]{3,2,1,0:T(4,128)(2,1)}, bf16[2048,256]{1,0:T(8,128)(2,1)S(1)}) %tuple.23, (bf16[256,8,4,1024]{3,2,1,0:T(4,128)(2,1)}, bf16[2048,256]{1,0:T(8,128)(2,1)S(1)}) %tuple.23), branch_computations={%region_1.2_spmd, %region_2.3_spmd} | conditional | flops 1073741824 | bytes 39321608
  64.6 12.4 %copy.27 = bf16[256,8,4,1024]{3,1,0,2:T(8,128)(2,1)S(1)} copy(bf16[256,8,4,1024]{3,2,1,0:T(4,128)(2,1)} %get-tuple-element.71) | data formatting | bytes 33554432 | tf_op jit(solution)/shard_map
  77.0 2.1 %fusion = bf16[1024,256]{1,0:T(8,128)(2,1)} fusion(bf16[2048,256]{1,0:T(8,128)(2,1)S(1)} %get-tuple-element.32, bf16[256,8,4,1024]{3,1,0,2:T(8,128)(2,1)S(1)} %copy.27), kind=kOutput, calls=%fused_computation.1 | convolution fusion | flops 1073741824 | bytes 5767168 | tf_op jit(solution)/shard_map/cond/branch_0_fun/ct,cb->tb/dot_general | solution.py:68
  79.1 0.0 all-to-all-done.2
  79.1 5.8 %all-to-all-start.1 = ((bf16[32,32,256]{2,1,0:T(8,128)(2,1)}), bf16[32,32,256]{2,1,0:T(8,128)(2,1)S(1)}, u32[]{:S(2)}, u32[]{:S(2)}) async-start(bf16[32,32,256]{2,1,0:T(8,128)(2,1)} %bitcast.8), calls=%async_computation.1 | async-start | bytes 1048576 | tf_op jit(solution)/shard_map/all_to_all | solution.py:129
  84.9 0.1 convert_reduce_fusion
  85.0 15.5 %all-to-all-done.1 = bf16[32,32,256]{2,1,0:T(8,128)(2,1)S(1)} async-done(((bf16[32,32,256]{2,1,0:T(8,128)(2,1)}), bf16[32,32,256]{2,1,0:T(8,128)(2,1)S(1)}, u32[]{:S(2)}, u32[]{:S(2)}) %all-to-all-start.1) | async-done | bytes 524320 | tf_op jit(solution)/shard_map/all_to_all | solution.py:129
  100.6 0.1 convert_reduce_fusion.1
  100.7 0.7 copy.32
  (6 shorter events, 0.1 us)
Async XLA Ops:
  5.0 19.0 %all-to-all-start = ((bf16[16,8,1152]{2,1,0:T(8,128)(2,1)}), bf16[16,8,1152]{2,1,0:T(8,128)(2,1)S(1)}, u32[]{:S(2)}, u32[]{:S(2)}) async-start(bf16[16,8,1152]{2,1,0:T(8,128)(2,1)} %fusion.4), calls=%async_computation | async-start | bytes 589824 | tf_op jit(solution)/shard_map/all_to_all | solution.py:105
  52.1 27.0 %all-to-all-start.2 = ((bf16[32,32,256]{2,1,0:T(8,128)(2,1)}), bf16[32,32,256]{2,1,0:T(8,128)(2,1)S(1)}, u32[]{:S(2)}, u32[]{:S(2)}) async-start(bf16[32,32,256]{2,1,0:T(8,128)(2,1)} %bitcast.12), calls=%async_computation.2 | async-start | bytes 1048576 | tf_op jit(solution)/shard_map/all_to_all | solution.py:129
  79.1 21.5 %all-to-all-start.1 = ((bf16[32,32,256]{2,1,0:T(8,128)(2,1)}), bf16[32,32,256]{2,1,0:T(8,128)(2,1)S(1)}, u32[]{:S(2)}, u32[]{:S(2)}) async-start(bf16[32,32,256]{2,1,0:T(8,128)(2,1)} %bitcast.8), calls=%async_computation.1 | async-start | bytes 1048576 | tf_op jit(solution)/shard_map/all_to_all | solution.py:129

commit v3 on v1

--- a/solution.py
+++ b/solution.py
@@ -108,7 +108,9 @@
     src = row_sources.reshape(rows_here * terms, panels)
     per = blocks // columns
     first = lax.axis_index("gy") * per
-    gains = lax.dynamic_slice_in_dim(gain_table, first, per, 2)
+    gains = lax.optimization_barrier(
+        gain_table.transpose(2, 0, 1, 3).reshape(blocks, rows_here * terms, observers)
+    )
     sums = []
     share = observers // (shards * columns)
     for o in range(per):
@@ -116,7 +118,7 @@
         arrived = bin_rows(block, src, arrival_bins, arrival_fracs)
         partial = jnp.einsum(
             "ct,cb->tb",
-            gains[:, :, o, :].reshape(rows_here * terms, observers),
+            lax.dynamic_index_in_dim(gains, first + o, 0, keepdims=False),
             arrived,
             preferred_element_type=jnp.float32,
         ).astype(jnp.bfloat16)

time: 105 us -> 93.8 us (0.89)
  local copies, waits for them, and re-layouts: 25.5 us -> 18.8 us
  matrix products: 15.4 us -> 10.5 us
    slice x1 -> x0, local copies, waits for them, and re-layouts: 23.7 us -> none  [on_device(): gains[:, :, o, :].reshape(rows_here * terms, observers)]
    transpose x0 -> x1, local copies, waits for them, and re-layouts: none -> 17 us  [on_device(): gain_table.transpose(2, 0, 1, 3)]
    dot_general x2, matrix products: 14.2 us -> 9.21 us  [on_device(): jnp.einsum('ct,cb->tb', lax.dynamic_index_in_dim(gains, first + o, 0, kee...]
  transfers between devices with their start and end apart: 3 -> 3, of which waited for: 1 -> 2; matrix products, arithmetic and copies ran while one was open for 29% -> 23% of each run, Pallas kernels for 10% -> 12%
where the time goes in v3:
time: 93.8 us; the launch traced here: 93.3 us
  Pallas kernels  21.7 us (23%)
  starting transfers between devices  19.9 us (21%)
  local copies, waits for them, and re-layouts  18.8 us (20%)
  waiting for transfers between devices  15.7 us (17%)
  matrix products  10.5 us (11%)
  other arithmetic  4.38 us (5%)
  blocking collectives  2.22 us (2%)
    pallas_call x2, Pallas kernels, bin_rows(): pl.pallas_call(bin_kernel, out_shape=jax.ShapeDtypeStruct((rows, NBIN), j...  21.7 us
    transpose x1, local copies, waits for them, and re-layouts, on_device(): gain_table.transpose(2, 0, 1, 3)  17 us
    all_to_all x2, waiting for transfers between devices, on_device(): lax.all_to_all(partial, ('gx', 'gy'), split_axis=0, concat_axis=0, tiled=...  15.7 us
    all_to_all x2, starting transfers between devices, on_device(): lax.all_to_all(partial, ('gx', 'gy'), split_axis=0, concat_axis=0, tiled=...  11.6 us
    dot_general x2, matrix products, on_device(): jnp.einsum('ct,cb->tb', lax.dynamic_index_in_dim(gains, first + o, 0, kee...  9.21 us
    all_to_all x1, starting transfers between devices, on_device(): got = lax.all_to_all(send, 'gx', split_axis=0, concat_axis=0, tiled=True)  8.35 us
    all_gather x1, blocking collectives, on_device(): got = lax.all_gather(got, 'gy', axis=0, tiled=True)  2.22 us
  transfers between devices with their start and end apart: 3, of which 2 were waited for; matrix products, arithmetic and copies ran while one was open for 23% of the time, Pallas kernels for 12%

profile of v3, /device:TPU:0, one launch (start us, length us, event | category | flops | bytes accessed | tf_op | source)
XLA Modules:
  0.0 93.3 jit_solution(5781376190806400912)
XLA Ops:
  0.0 0.7 and_select_fusion.1
  0.7 0.7 fusion.22
  1.4 0.9 broadcast_multiply_fusion
  2.4 0.9 select_reduce_fusion
  3.3 0.7 multiply_add_fusion
  3.9 0.1 select_convert_fusion
  4.0 0.9 fusion.6
  5.0 8.3 %all-to-all-start = ((bf16[16,8,1152]{2,1,0:T(8,128)(2,1)}), bf16[16,8,1152]{2,1,0:T(8,128)(2,1)S(1)}, u32[]{:S(2)}, u32[]{:S(2)}) async-start(bf16[16,8,1152]{2,1,0:T(8,128)(2,1)} %fusion.6), calls=%async_computation | async-start | bytes 589824 | tf_op jit(solution)/shard_map/all_to_all | solution.py:98
  13.3 17.0 %copy.21 = bf16[4,256,8,1024]{3,2,1,0:T(8,128)(2,1)} copy(bf16[4,256,8,1024]{3,0,2,1:T(4,128)(2,1)} %bitcast.38) | data formatting | bytes 33554432 | tf_op jit(solution)/shard_map/transpose | solution.py:112
  30.3 0.0 all-to-all-done
  30.3 2.2 %all_gather.3 = bf16[256,1152]{1,0:T(8,128)(2,1)S(1)} all-gather(bf16[128,1152]{1,0:T(8,128)(2,1)S(1)} %bitcast.43), channel_id=1, replica_groups=mesh['gx'=16,'gy'=2] {'gy'}, dimensions={0}, use_global_device_ids=true | all-gather | bytes 884736 | tf_op jit(solution)/shard_map/all_gather | solution.py:99
  32.5 0.2 fusion.18
  32.8 0.3 convolution_convert_fusion.1
  33.1 1.0 %reshape.104.src_ref = bf16[2048,128]{1,0:T(8,128)(2,1)} reshape(bf16[256,1024]{1,0:T(8,128)(2,1)S(1)} %convolution_convert_fusion.1) | data formatting | bytes 1048576 | tf_op jit(solution)/shard_map/reshape | solution.py:108
  34.1 10.9 %bin_rows.3 = bf16[2048,256]{1,0:T(8,128)(2,1)} custom-call(s32[1]{0:T(128)} %bitcast.11.block_ref, bf16[2048,128]{1,0:T(8,128)(2,1)} %reshape.104.src_ref, s32[256,4,128]{2,1,0:T(4,128)} %bins_ref.3, f32[256,4,128]{2,1,0:T(4,128)} %fracs_ref.3), custom_call_target="tpu_custom_call" | custom-call | flops 268435456 | bytes 2048000 | tf_op jit(solution)/shard_map/bin_rows/pallas_call | solution.py:51
  45.0 4.6 %fusion.10 = bf16[1024,256]{1,0:T(8,128)(2,1)} fusion(bf16[2048,256]{1,0:T(8,128)(2,1)} %bin_rows.3, bf16[4,2048,1024]{2,1,0:T(8,128)(2,1)} %bitcast.39, s32[]{:T(128)S(6)} %select_n.60), kind=kOutput, calls=%fused_computation.11 | convolution fusion | flops 1074003968 | bytes 5767172 | tf_op jit(solution)/shard_map/ct,cb->tb/dot_general | solution.py:119
  49.6 5.9 %all-to-all-start.2 = ((bf16[32,32,256]{2,1,0:T(8,128)(2,1)}), bf16[32,32,256]{2,1,0:T(8,128)(2,1)S(1)}, u32[]{:S(2)}, u32[]{:S(2)}) async-start(bf16[32,32,256]{2,1,0:T(8,128)(2,1)} %bitcast.12), calls=%async_computation.2 | async-start | bytes 1048576 | tf_op jit(solution)/shard_map/all_to_all | solution.py:125
  55.5 10.9 %bin_rows.2 = bf16[2048,256]{1,0:T(8,128)(2,1)} custom-call(s32[1]{0:T(128)} %bitcast.3.block_ref, bf16[2048,128]{1,0:T(8,128)(2,1)} %reshape.104.src_ref, s32[256,4,128]{2,1,0:T(4,128)} %bins_ref.3, f32[256,4,128]{2,1,0:T(4,128)} %fracs_ref.3), custom_call_target="tpu_custom_call" | custom-call | flops 268435456 | bytes 2048000 | tf_op jit(solution)/shard_map/bin_rows/pallas_call | solution.py:51
  66.4 4.6 %fusion.7 = bf16[1024,256]{1,0:T(8,128)(2,1)} fusion(bf16[2048,256]{1,0:T(8,128)(2,1)} %bin_rows.2, bf16[4,2048,1024]{2,1,0:T(8,128)(2,1)} %bitcast.40, s32[]{:T(128)S(6)} %select_n.51), kind=kOutput, calls=%fused_computation.10 | convolution fusion | flops 1074003968 | bytes 5767172 | tf_op jit(solution)/shard_map/ct,cb->tb/dot_general | solution.py:119
  71.0 0.1 all-to-all-done.2
  71.1 5.7 %all-to-all-start.1 = ((bf16[32,32,256]{2,1,0:T(8,128)(2,1)}), bf16[32,32,256]{2,1,0:T(8,128)(2,1)S(1)}, u32[]{:S(2)}, u32[]{:S(2)}) async-start(bf16[32,32,256]{2,1,0:T(8,128)(2,1)} %bitcast.7), calls=%async_computation.1 | async-start | bytes 1048576 | tf_op jit(solution)/shard_map/all_to_all | solution.py:125
  76.8 0.1 convert_reduce_fusion
  76.9 15.5 %all-to-all-done.1 = bf16[32,32,256]{2,1,0:T(8,128)(2,1)S(1)} async-done(((bf16[32,32,256]{2,1,0:T(8,128)(2,1)}), bf16[32,32,256]{2,1,0:T(8,128)(2,1)S(1)}, u32[]{:S(2)}, u32[]{:S(2)}) %all-to-all-start.1) | async-done | bytes 524320 | tf_op jit(solution)/shard_map/all_to_all | solution.py:125
  92.4 0.1 convert_reduce_fusion.1
  92.5 0.7 copy.17
  (6 shorter events, 0.1 us)
Async XLA Ops:
  5.0 25.3 %all-to-all-start = ((bf16[16,8,1152]{2,1,0:T(8,128)(2,1)}), bf16[16,8,1152]{2,1,0:T(8,128)(2,1)S(1)}, u32[]{:S(2)}, u32[]{:S(2)}) async-start(bf16[16,8,1152]{2,1,0:T(8,128)(2,1)} %fusion.6), calls=%async_computation | async-start | bytes 589824 | tf_op jit(solution)/shard_map/all_to_all | solution.py:98
  49.6 21.5 %all-to-all-start.2 = ((bf16[32,32,256]{2,1,0:T(8,128)(2,1)}), bf16[32,32,256]{2,1,0:T(8,128)(2,1)S(1)}, u32[]{:S(2)}, u32[]{:S(2)}) async-start(bf16[32,32,256]{2,1,0:T(8,128)(2,1)} %bitcast.12), calls=%async_computation.2 | async-start | bytes 1048576 | tf_op jit(solution)/shard_map/all_to_all | solution.py:125
  71.1 21.3 %all-to-all-start.1 = ((bf16[32,32,256]{2,1,0:T(8,128)(2,1)}), bf16[32,32,256]{2,1,0:T(8,128)(2,1)S(1)}, u32[]{:S(2)}, u32[]{:S(2)}) async-start(bf16[32,32,256]{2,1,0:T(8,128)(2,1)} %bitcast.7), calls=%async_computation.1 | async-start | bytes 1048576 | tf_op jit(solution)/shard_map/all_to_all | solution.py:125
